TPU v7x, 256 devices: a whole 4x4x8 slice. The times are simulated.
256 devices in a mesh: lat: 8 (over z), lon: 16 (over x, y), obs: 2 (over core).
Axes of the slice: x: 4, y: 4, z: 8, core: 2. Of those that a mesh axis runs over, the one named last changes fastest.
Arguments:
- innovation: float32 [32768, 128], P(('lat', 'lon', 'obs')), may hold values from -6 to 6
- obs_error: float32 [32768, 128], P(('lat', 'lon', 'obs')), may hold values from 0.5 to 2
- obs_offset: float32 [2, 32768, 128], P(None, ('lat', 'lon', 'obs')), may hold values from 0 to 1
- obs_cell: int32 [32768, 128], P(('lat', 'lon', 'obs')), may hold values from 0 to 65535
- obs_owner: int32 [256, 128], P(('lat', 'lon', 'obs')), may hold values from 0 to 127, as said below
- block_count: int32 [256], P(('lat', 'lon', 'obs')), may hold values from 64 to 128
- land_mask: int32 [512, 16384], P(('lat', 'obs'), 'lon'), may hold values from 0 to 1, as said below
- inertia: float32 [512, 16384], P(('lat', 'obs'), 'lon'), may hold values from 0.002 to 0.05
- sea_depth: float32 [512, 16384], P(('lat', 'obs'), 'lon'), may hold values from 0.5 to 5
Outputs:
- adjoint_field: float32 [512, 16384], P(('lat', 'obs'), 'lon')
- residual: float32 [512, 16384], P(('lat', 'obs'), 'lon')
Inputs may be any that keep to these rules, and one draw needn't show every extreme that they name: `obs_owner`: among the live blocks of one device at most 3 name the same tile; in every draw some tile is named by exactly 3 live blocks of every device. `land_mask`: the first and the last grid row are land.
All inputs are finite; a program needn't handle non-finite values.
Results may differ from a plain program's by a relative error of at most 0.0003.
Values sent between devices are 32-bit elements; how exact they have to be, the bound alone decides.
No kernel may reach another device: no remote copies, remote signals or barrier semaphores. Data moves between devices by JAX's collectives and lax.ppermute only.
A program may use at most 64 MiB of HBM per device.

v0:
```python
import jax
import jax.numpy as jnp
from jax import lax
from jax.sharding import Mesh
from jax.sharding import PartitionSpec as P

ITERS = 5
LON = ("lon_0", "lon_1")
LAT_LON_OBS = ("lat", "lon_0", "lon_1", "obs")
LAT_LON = ("lat", "lon_0", "lon_1")


def extended(block, sides, width):
    for axis, dim in sides:
        count = lax.axis_size(axis)
        forward = [(i, i + 1) for i in range(count - 1)]
        forward.append((count - 1, 0))
        backward = [(target, source) for source, target in forward]
        low = lax.ppermute(
            lax.slice_in_dim(block, block.shape[dim] - width, None, axis=dim), axis, forward
        )
        high = lax.ppermute(lax.slice_in_dim(block, 0, width, axis=dim), axis, backward)
        block = jnp.concatenate([low, block, high], axis=dim)
    return block


def by_axis(value, axes):
    for axis in axes:
        value = lax.psum(value, axis)
    return value


def cut_along(value, dim, peers):
    shape = value.shape
    tiles = value.reshape(*shape[:dim], peers, shape[dim] // peers, *shape[dim + 1 :])
    return jnp.moveaxis(tiles, dim, 0)


def in_order(tiles, dim):
    tiles = jnp.moveaxis(tiles, 0, dim)
    shape = tiles.shape
    return tiles.reshape(*shape[:dim], shape[dim] * shape[dim + 1], *shape[dim + 2 :])


def exchange_both(value, axis, axes, splits, concats):
    sizes = [lax.axis_size(a) for a in axes]
    tiles = cut_along(value, splits[0], sizes[0])
    tiles = jnp.moveaxis(cut_along(tiles, splits[1] + 1, sizes[1]), 0, 1)
    inside = tiles.shape[2:]
    tiles = tiles.reshape(-1, *inside)
    tiles = lax.all_to_all(tiles, axis, split_axis=0, concat_axis=0, tiled=True)
    tiles = in_order(tiles.reshape(*sizes, *inside), concats[0] + 1)
    return in_order(tiles, concats[1])


def shifted(value, axis, steps):
    count = lax.axis_size(axis)
    pairs = [(source, (source + steps) % count) for source in range(count)]
    return lax.ppermute(value, axis, pairs)


def shifted_2(block, axis, distance):
    devices = range(lax.axis_size(axis))
    route = [(i - distance, i) for i in devices if i - distance in devices]
    return lax.ppermute(block, axis, route)


def sent_and_summed(value, axis, dim):
    tiles = cut_along(value, dim, lax.axis_size(axis))
    arrived = lax.all_to_all(tiles, axis, split_axis=0, concat_axis=0, tiled=True)
    return arrived.sum(axis=0)


def border(field):
    return extended(field, ((("lat", "obs"), 0), (LON, 1)), 1)


def two_products(residual, applied):
    return (
        by_axis(jnp.sum(residual * residual), LAT_LON_OBS),
        by_axis(jnp.sum(residual * applied), LAT_LON_OBS),
    )


def body(
    innovation,
    obs_error,
    obs_offset,
    obs_cell,
    obs_owner,
    block_count,
    land_mask,
    inertia,
    sea_depth,
):
    block_total = obs_owner.shape[1]
    block_width = innovation.shape[1]
    n_lat = lax.axis_size("lat")
    n_lon = lax.axis_size(LON)
    tile_count = n_lat * n_lon
    capacity = max(3, 2 * ((block_total + tile_count - 1) // tile_count))
    slot_total = tile_count * capacity
    tile_rows = land_mask.shape[0] * lax.axis_size("obs")
    tile_cols = land_mask.shape[1]
    owners = obs_owner[0]
    block_ids = jnp.arange(block_total)
    is_live = block_ids < block_count[0]
    earlier = block_ids[None, :] < block_ids[:, None]
    same_owner = (owners[None, :] == owners[:, None]) & earlier & is_live[None, :]
    slot_rank = jnp.sum(same_owner.astype(jnp.int32), axis=1)
    target = jnp.where(is_live, owners * capacity + slot_rank, slot_total)
    scaled = innovation / (obs_error * obs_error)
    floats = jnp.stack([scaled, obs_offset[0], obs_offset[1]], axis=1)

    def put_slots(values):
        holder = jnp.zeros((slot_total + 1,) + values.shape[1:], values.dtype)
        return holder.at[target].set(values)[:slot_total]

    sent_floats = put_slots(floats)
    sent_cells = put_slots(obs_cell)
    received, cell_ids = (
        exchange_both(
            sent_floats.reshape(n_lat, n_lon, capacity, 3, block_width),
            LAT_LON,
            ("lat", LON),
            (0, 1),
            (0, 1),
        ),
        exchange_both(
            sent_cells.reshape(n_lat, n_lon, capacity, block_width),
            LAT_LON,
            ("lat", LON),
            (0, 1),
            (0, 1),
        ),
    )
    received = received.reshape(-1, 3, block_width)
    cell_ids = cell_ids.reshape(-1, block_width)
    group = 1
    for size_try in range(1, slot_total + 1):
        if slot_total % size_try == 0 and size_try * block_width <= 4096:
            group = size_try
    turns = slot_total // group
    group_obs = group * block_width
    scaled_in = received[:, 0].reshape(turns, group_obs)
    north_frac = received[:, 1].reshape(turns, group_obs)
    east_frac = received[:, 2].reshape(turns, group_obs)
    cells_in = cell_ids.reshape(turns, group_obs)
    wide = tile_cols + 1
    row_axis = jnp.arange(tile_rows + 1, dtype=jnp.int32)[:, None]
    col_axis = jnp.arange(wide, dtype=jnp.int32)[None, :]

    def spread(total, pieces):
        amount, north, east, cells = pieces
        cell_row = (cells // tile_cols)[None, :]
        cell_col = (cells % tile_cols)[:, None]
        row_weights = (
            jnp.where(row_axis == cell_row, 1.0 - north[None, :], 0.0)
            + jnp.where(row_axis == cell_row + 1, north[None, :], 0.0)
        ) * amount[None, :]
        col_weights = jnp.where(col_axis == cell_col, 1.0 - east[:, None], 0.0) + jnp.where(
            col_axis == cell_col + 1, east[:, None], 0.0
        )
        return (
            total
            + jnp.dot(
                row_weights,
                col_weights,
                precision=lax.Precision.HIGHEST,
                preferred_element_type=jnp.float32,
            ),
            None,
        )

    partial_value, unused = lax.scan(
        spread,
        jnp.zeros((tile_rows + 1, wide), jnp.float32),
        (scaled_in, north_frac, east_frac, cells_in),
    )
    arrived_col = shifted(partial_value[:, tile_cols], LON, 1)
    partial_value = partial_value[:, :tile_cols].at[:, 0].add(arrived_col)
    arrived_row = shifted_2(partial_value[tile_rows], "lat", 1)
    tile_part = partial_value[:tile_rows].at[0].add(arrived_row)
    ocean = land_mask.astype(jnp.float32)
    forcing = sent_and_summed(tile_part, "obs", 0) * ocean
    conduct = ocean * sea_depth
    padded = border(conduct)
    cond_north = jnp.sqrt(conduct * padded[:-2, 1:-1])
    cond_south = jnp.sqrt(conduct * padded[2:, 1:-1])
    cond_west = jnp.sqrt(conduct * padded[1:-1, :-2])
    cond_east = jnp.sqrt(conduct * padded[1:-1, 2:])
    diagonal = inertia + cond_north + cond_south + cond_west + cond_east

    def operate(field):
        outer = border(field)
        return (
            diagonal * field
            - cond_north * outer[:-2, 1:-1]
            - cond_south * outer[2:, 1:-1]
            - cond_west * outer[1:-1, :-2]
            - cond_east * outer[1:-1, 2:]
        )

    adjoint_field = jnp.zeros_like(forcing)
    residual = forcing
    applied = operate(residual)
    norm_now, product = two_products(residual, applied)
    step_size = norm_now / product
    direction = residual
    applied_dir = applied
    for iteration in range(ITERS):
        adjoint_field = adjoint_field + step_size * direction
        residual = residual - step_size * applied_dir
        if iteration + 1 < ITERS:
            applied = operate(residual)
            norm_next, product = two_products(residual, applied)
            beta_ratio = norm_next / norm_now
            step_size = norm_next / (product - beta_ratio * norm_next / step_size)
            direction = residual + beta_ratio * direction
            applied_dir = applied + beta_ratio * applied_dir
            norm_now = norm_next
    return (adjoint_field, residual)


def solution(mesh):
    split = Mesh(
        mesh.devices.reshape(mesh.shape["lat"], 4, 4, mesh.shape["obs"]),
        ("lat", "lon_0", "lon_1", "obs"),
    )
    return jax.shard_map(
        body,
        mesh=split,
        in_specs=(
            P(LAT_LON_OBS, None),
            P(LAT_LON_OBS, None),
            P(None, LAT_LON_OBS, None),
            P(LAT_LON_OBS, None),
            P(LAT_LON_OBS, None),
            P(LAT_LON_OBS),
            P(("lat", "obs"), LON),
            P(("lat", "obs"), LON),
            P(("lat", "obs"), LON),
        ),
        out_specs=(P(("lat", "obs"), LON), P(("lat", "obs"), LON)),
        check_vma=False,
    )
```

profile of v0, /device:TPU:1, one launch (start us, length us, event | category | flops | bytes accessed | tf_op | source)
XLA Modules:
  0.0 609.3 jit_solution(17351134791260999394)
XLA Ops:
  2.9 1.2 scatter_custom_fusion
  4.8 16.3 %all-to-all-start = ((s32[128,1,1,3,128]{4,2,3,1,0:T(1,128)}), s32[128,1,1,3,128]{4,2,3,1,0:T(1,128)S(1)}, u32[]{:S(2)}, u32[]{:S(2)}) async-start(s32[128,1,1,3,128]{4,2,3,1,0:T(1,128)} %bitcast.5), calls=%async_computation | async-start | bytes 393216 | tf_op jit(solution)/shard_map/all_to_all | solution.py:51
  21.5 4.5 scatter_fusion
  26.2 1.4 copy.29
  27.6 5.6 all-to-all-done
  33.1 7.6 %all-to-all-start.1 = ((f32[128,1,1,3,3,128]{5,2,4,3,1,0:T(1,128)}), f32[128,1,1,3,3,128]{5,2,4,3,1,0:T(1,128)S(1)}, u32[]{:S(2)}, u32[]{:S(2)}) async-start(f32[128,1,1,3,3,128]{5,2,4,3,1,0:T(1,128)} %copy.29), calls=%async_computation.1 | async-start | bytes 1179648 | tf_op jit(solution)/shard_map/all_to_all | solution.py:51
  40.9 19.1 %all-to-all-done.1 = f32[128,1,1,3,3,128]{5,2,4,3,1,0:T(1,128)S(1)} async-done(((f32[128,1,1,3,3,128]{5,2,4,3,1,0:T(1,128)}), f32[128,1,1,3,3,128]{5,2,4,3,1,0:T(1,128)S(1)}, u32[]{:S(2)}, u32[]{:S(2)}) %all-to-all-start.1) | async-done | bytes 589856 | tf_op jit(solution)/shard_map/all_to_all | solution.py:51
  60.7 236.9 %while.16 = (s32[]{:T(128)}, f32[65,1025]{1,0:T(8,128)S(1)}, s32[12,4096]{1,0:T(8,128)S(1)}, f32[12,4096]{1,0:T(8,128)S(1)}, f32[12,4096]{1,0:T(8,128)S(1)}, /*index=5*/f32[12,4096]{1,0:T(8,128)S(1)}, s32[]{:T(128)}, s32[]{:T(128)}) while((s32[]{:T(128)}, f32[65,1025]{1,0:T(8,128)S(1)}, s32[12,4096]{1,0:T(8,128)S(1)}, ...), condition=%wide.region_4.5_spmd.clone.clone, body=%wide.region_3.4_spmd.clone.clone.sunk | while | flops 3297597440 | bytes 942707 | solution.py:175
  61.3 18.7 %fusion.98 = f32[65,1025]{1,0:T(8,128)S(1)} fusion(f32[4096]{0:T(1024)S(1)} %bitcast.80, s32[4096]{0:T(1024)S(1)} %get-tuple-element.342, f32[4096]{0:T(1024)S(1)} %broadcast_subtract_fusion.5, s32[4096]{0:T(1024)S(1)} %get-tuple-element.343, f32[4096]{0:T(1024)S(1)} %bitcast.87, f32[4096]{0:T(1024)S(1)} %bitcast.86, s32[4096]{0:T(1024)S(1)} %bitcast.88, ...), kind=kOutput, calls=%fused_computation.15.clone.1 | convolution fusion | flops 3297474560 | bytes 680457 | tf_op jit(solution)/shard_map/while/body/eval_jaxpr/dot_general | solution.py:166
  80.3 18.7 %fusion.98 = f32[65,1025]{1,0:T(8,128)S(1)} fusion(f32[4096]{0:T(1024)S(1)} %bitcast.80, s32[4096]{0:T(1024)S(1)} %get-tuple-element.342, f32[4096]{0:T(1024)S(1)} %broadcast_subtract_fusion.5, s32[4096]{0:T(1024)S(1)} %get-tuple-element.343, f32[4096]{0:T(1024)S(1)} %bitcast.87, f32[4096]{0:T(1024)S(1)} %bitcast.86, s32[4096]{0:T(1024)S(1)} %bitcast.88, ...), kind=kOutput, calls=%fused_computation.15.clone.1 | convolution fusion | flops 3297474560 | bytes 680457 | tf_op jit(solution)/shard_map/while/body/eval_jaxpr/dot_general | solution.py:166
  99.3 18.7 %fusion.98 = f32[65,1025]{1,0:T(8,128)S(1)} fusion(f32[4096]{0:T(1024)S(1)} %bitcast.80, s32[4096]{0:T(1024)S(1)} %get-tuple-element.342, f32[4096]{0:T(1024)S(1)} %broadcast_subtract_fusion.5, s32[4096]{0:T(1024)S(1)} %get-tuple-element.343, f32[4096]{0:T(1024)S(1)} %bitcast.87, f32[4096]{0:T(1024)S(1)} %bitcast.86, s32[4096]{0:T(1024)S(1)} %bitcast.88, ...), kind=kOutput, calls=%fused_computation.15.clone.1 | convolution fusion | flops 3297474560 | bytes 680457 | tf_op jit(solution)/shard_map/while/body/eval_jaxpr/dot_general | solution.py:166
  118.3 18.7 %fusion.98 = f32[65,1025]{1,0:T(8,128)S(1)} fusion(f32[4096]{0:T(1024)S(1)} %bitcast.80, s32[4096]{0:T(1024)S(1)} %get-tuple-element.342, f32[4096]{0:T(1024)S(1)} %broadcast_subtract_fusion.5, s32[4096]{0:T(1024)S(1)} %get-tuple-element.343, f32[4096]{0:T(1024)S(1)} %bitcast.87, f32[4096]{0:T(1024)S(1)} %bitcast.86, s32[4096]{0:T(1024)S(1)} %bitcast.88, ...), kind=kOutput, calls=%fused_computation.15.clone.1 | convolution fusion | flops 3297474560 | bytes 680457 | tf_op jit(solution)/shard_map/while/body/eval_jaxpr/dot_general | solution.py:166
  137.3 18.7 %fusion.98 = f32[65,1025]{1,0:T(8,128)S(1)} fusion(f32[4096]{0:T(1024)S(1)} %bitcast.80, s32[4096]{0:T(1024)S(1)} %get-tuple-element.342, f32[4096]{0:T(1024)S(1)} %broadcast_subtract_fusion.5, s32[4096]{0:T(1024)S(1)} %get-tuple-element.343, f32[4096]{0:T(1024)S(1)} %bitcast.87, f32[4096]{0:T(1024)S(1)} %bitcast.86, s32[4096]{0:T(1024)S(1)} %bitcast.88, ...), kind=kOutput, calls=%fused_computation.15.clone.1 | convolution fusion | flops 3297474560 | bytes 680457 | tf_op jit(solution)/shard_map/while/body/eval_jaxpr/dot_general | solution.py:166
  156.2 18.7 %fusion.98 = f32[65,1025]{1,0:T(8,128)S(1)} fusion(f32[4096]{0:T(1024)S(1)} %bitcast.80, s32[4096]{0:T(1024)S(1)} %get-tuple-element.342, f32[4096]{0:T(1024)S(1)} %broadcast_subtract_fusion.5, s32[4096]{0:T(1024)S(1)} %get-tuple-element.343, f32[4096]{0:T(1024)S(1)} %bitcast.87, f32[4096]{0:T(1024)S(1)} %bitcast.86, s32[4096]{0:T(1024)S(1)} %bitcast.88, ...), kind=kOutput, calls=%fused_computation.15.clone.1 | convolution fusion | flops 3297474560 | bytes 680457 | tf_op jit(solution)/shard_map/while/body/eval_jaxpr/dot_general | solution.py:166
  175.2 18.7 %fusion.98 = f32[65,1025]{1,0:T(8,128)S(1)} fusion(f32[4096]{0:T(1024)S(1)} %bitcast.80, s32[4096]{0:T(1024)S(1)} %get-tuple-element.342, f32[4096]{0:T(1024)S(1)} %broadcast_subtract_fusion.5, s32[4096]{0:T(1024)S(1)} %get-tuple-element.343, f32[4096]{0:T(1024)S(1)} %bitcast.87, f32[4096]{0:T(1024)S(1)} %bitcast.86, s32[4096]{0:T(1024)S(1)} %bitcast.88, ...), kind=kOutput, calls=%fused_computation.15.clone.1 | convolution fusion | flops 3297474560 | bytes 680457 | tf_op jit(solution)/shard_map/while/body/eval_jaxpr/dot_general | solution.py:166
  194.2 18.7 %fusion.98 = f32[65,1025]{1,0:T(8,128)S(1)} fusion(f32[4096]{0:T(1024)S(1)} %bitcast.80, s32[4096]{0:T(1024)S(1)} %get-tuple-element.342, f32[4096]{0:T(1024)S(1)} %broadcast_subtract_fusion.5, s32[4096]{0:T(1024)S(1)} %get-tuple-element.343, f32[4096]{0:T(1024)S(1)} %bitcast.87, f32[4096]{0:T(1024)S(1)} %bitcast.86, s32[4096]{0:T(1024)S(1)} %bitcast.88, ...), kind=kOutput, calls=%fused_computation.15.clone.1 | convolution fusion | flops 3297474560 | bytes 680457 | tf_op jit(solution)/shard_map/while/body/eval_jaxpr/dot_general | solution.py:166
  213.2 18.7 %fusion.98 = f32[65,1025]{1,0:T(8,128)S(1)} fusion(f32[4096]{0:T(1024)S(1)} %bitcast.80, s32[4096]{0:T(1024)S(1)} %get-tuple-element.342, f32[4096]{0:T(1024)S(1)} %broadcast_subtract_fusion.5, s32[4096]{0:T(1024)S(1)} %get-tuple-element.343, f32[4096]{0:T(1024)S(1)} %bitcast.87, f32[4096]{0:T(1024)S(1)} %bitcast.86, s32[4096]{0:T(1024)S(1)} %bitcast.88, ...), kind=kOutput, calls=%fused_computation.15.clone.1 | convolution fusion | flops 3297474560 | bytes 680457 | tf_op jit(solution)/shard_map/while/body/eval_jaxpr/dot_general | solution.py:166
  232.2 18.7 %fusion.98 = f32[65,1025]{1,0:T(8,128)S(1)} fusion(f32[4096]{0:T(1024)S(1)} %bitcast.80, s32[4096]{0:T(1024)S(1)} %get-tuple-element.342, f32[4096]{0:T(1024)S(1)} %broadcast_subtract_fusion.5, s32[4096]{0:T(1024)S(1)} %get-tuple-element.343, f32[4096]{0:T(1024)S(1)} %bitcast.87, f32[4096]{0:T(1024)S(1)} %bitcast.86, s32[4096]{0:T(1024)S(1)} %bitcast.88, ...), kind=kOutput, calls=%fused_computation.15.clone.1 | convolution fusion | flops 3297474560 | bytes 680457 | tf_op jit(solution)/shard_map/while/body/eval_jaxpr/dot_general | solution.py:166
  251.2 18.7 %fusion.98 = f32[65,1025]{1,0:T(8,128)S(1)} fusion(f32[4096]{0:T(1024)S(1)} %bitcast.80, s32[4096]{0:T(1024)S(1)} %get-tuple-element.342, f32[4096]{0:T(1024)S(1)} %broadcast_subtract_fusion.5, s32[4096]{0:T(1024)S(1)} %get-tuple-element.343, f32[4096]{0:T(1024)S(1)} %bitcast.87, f32[4096]{0:T(1024)S(1)} %bitcast.86, s32[4096]{0:T(1024)S(1)} %bitcast.88, ...), kind=kOutput, calls=%fused_computation.15.clone.1 | convolution fusion | flops 3297474560 | bytes 680457 | tf_op jit(solution)/shard_map/while/body/eval_jaxpr/dot_general | solution.py:166
  270.2 18.7 %fusion.98 = f32[65,1025]{1,0:T(8,128)S(1)} fusion(f32[4096]{0:T(1024)S(1)} %bitcast.80, s32[4096]{0:T(1024)S(1)} %get-tuple-element.342, f32[4096]{0:T(1024)S(1)} %broadcast_subtract_fusion.5, s32[4096]{0:T(1024)S(1)} %get-tuple-element.343, f32[4096]{0:T(1024)S(1)} %bitcast.87, f32[4096]{0:T(1024)S(1)} %bitcast.86, s32[4096]{0:T(1024)S(1)} %bitcast.88, ...), kind=kOutput, calls=%fused_computation.15.clone.1 | convolution fusion | flops 3297474560 | bytes 680457 | tf_op jit(solution)/shard_map/while/body/eval_jaxpr/dot_general | solution.py:166
  299.0 4.5 collective-permute-done
  304.5 2.7 collective-permute-start.1
  308.0 9.0 %all_to_all.15 = f32[2,32,1024]{2,1,0:T(8,128)S(1)} all-to-all(f32[2,32,1024]{2,1,0:T(8,128)S(1)} %bitcast.83), channel_id=1, replica_groups=mesh['lat'=8,'lon_0'=4,'lon_1'=4,'obs'=2] {'obs'}, dimensions={0} | all-to-all | bytes 524288 | tf_op jit(solution)/shard_map/all_to_all | solution.py:70
  317.1 2.3 collective-permute-start.2
  319.4 1.7 collective-permute-start.6
  321.1 1.3 collective-permute-done.3
  322.5 4.8 collective-permute-start.5
  327.4 4.8 collective-permute-start.9
  334.3 13.2 %all-reduce.4 = (f32[]{:T(128)}, f32[]{:T(128)}) all-reduce(f32[]{:T(128)} %get-tuple-element.194, f32[]{:T(128)} %get-tuple-element.193), channel_id=1, replica_groups=mesh['lat'=8,'lon_0'=4,'lon_1'=4,'obs'=2] {'lat'}, use_global_device_ids=true, to_apply=%region_8.9 | all-reduce | flops 2 | bytes 16 | tf_op jit(solution)/shard_map/psum | solution.py:29
  347.5 6.6 %all-reduce.14 = (f32[]{:T(128)}, f32[]{:T(128)}) all-reduce(f32[]{:T(128)} %get-tuple-element.215, f32[]{:T(128)} %get-tuple-element.216), channel_id=1, replica_groups=mesh['lat'=8,'lon_0'=4,'lon_1'=4,'obs'=2] {'lon_0'}, use_global_device_ids=true, to_apply=%region_9.10 | all-reduce | flops 2 | bytes 16 | tf_op jit(solution)/shard_map/psum | solution.py:29
  354.1 11.7 %all-reduce.9 = (f32[]{:T(128)}, f32[]{:T(128)}) all-reduce(f32[]{:T(128)} %get-tuple-element.235, f32[]{:T(128)} %get-tuple-element.236), channel_id=1, replica_groups=mesh['lat'=8,'lon_0'=4,'lon_1'=4,'obs'=2] {'lon_1'}, use_global_device_ids=true, to_apply=%region_10.11 | all-reduce | flops 2 | bytes 16 | tf_op jit(solution)/shard_map/psum | solution.py:29
  365.7 11.4 %all-reduce.19 = (f32[]{:T(128)}, f32[]{:T(128)}) all-reduce(f32[]{:T(128)} %get-tuple-element.225, f32[]{:T(128)} %get-tuple-element.226), channel_id=1, replica_groups=mesh['lat'=8,'lon_0'=4,'lon_1'=4,'obs'=2] {'obs'}, use_global_device_ids=true, to_apply=%region_11.12 | all-reduce | flops 2 | bytes 16 | tf_op jit(solution)/shard_map/psum | solution.py:29
  378.5 2.0 collective-permute-start.10
  381.2 2.3 collective-permute-done.11
  383.6 4.8 collective-permute-start.13
  388.4 1.6 collective-permute-done.12
  390.9 13.4 %all-reduce.3 = (f32[]{:T(128)}, f32[]{:T(128)}) all-reduce(f32[]{:T(128)} %get-tuple-element.192, f32[]{:T(128)} %get-tuple-element.191), channel_id=1, replica_groups=mesh['lat'=8,'lon_0'=4,'lon_1'=4,'obs'=2] {'lat'}, use_global_device_ids=true, to_apply=%region_18.19 | all-reduce | flops 2 | bytes 16 | tf_op jit(solution)/shard_map/psum | solution.py:29
  404.3 6.7 %all-reduce.13 = (f32[]{:T(128)}, f32[]{:T(128)}) all-reduce(f32[]{:T(128)} %get-tuple-element.213, f32[]{:T(128)} %get-tuple-element.214), channel_id=1, replica_groups=mesh['lat'=8,'lon_0'=4,'lon_1'=4,'obs'=2] {'lon_0'}, use_global_device_ids=true, to_apply=%region_19.20 | all-reduce | flops 2 | bytes 16 | tf_op jit(solution)/shard_map/psum | solution.py:29
  411.0 11.9 %all-reduce.8 = (f32[]{:T(128)}, f32[]{:T(128)}) all-reduce(f32[]{:T(128)} %get-tuple-element.233, f32[]{:T(128)} %get-tuple-element.234), channel_id=1, replica_groups=mesh['lat'=8,'lon_0'=4,'lon_1'=4,'obs'=2] {'lon_1'}, use_global_device_ids=true, to_apply=%region_20.21 | all-reduce | flops 2 | bytes 16 | tf_op jit(solution)/shard_map/psum | solution.py:29
  422.9 9.6 %all-reduce.18 = (f32[]{:T(128)}, f32[]{:T(128)}) all-reduce(f32[]{:T(128)} %get-tuple-element.223, f32[]{:T(128)} %get-tuple-element.224), channel_id=1, replica_groups=mesh['lat'=8,'lon_0'=4,'lon_1'=4,'obs'=2] {'obs'}, use_global_device_ids=true, to_apply=%region_21.22 | all-reduce | flops 2 | bytes 16 | tf_op jit(solution)/shard_map/psum | solution.py:29
  437.1 1.2 collective-permute-start.14
  439.0 2.3 collective-permute-done.15
  441.4 4.8 collective-permute-start.17
  446.2 1.2 collective-permute-done.16
  448.3 14.4 %all-reduce.2 = (f32[]{:T(128)}, f32[]{:T(128)}) all-reduce(f32[]{:T(128)} %get-tuple-element.190, f32[]{:T(128)} %get-tuple-element.189), channel_id=1, replica_groups=mesh['lat'=8,'lon_0'=4,'lon_1'=4,'obs'=2] {'lat'}, use_global_device_ids=true, to_apply=%region_28.29 | all-reduce | flops 2 | bytes 16 | tf_op jit(solution)/shard_map/psum | solution.py:29
  462.7 6.6 %all-reduce.12 = (f32[]{:T(128)}, f32[]{:T(128)}) all-reduce(f32[]{:T(128)} %get-tuple-element.211, f32[]{:T(128)} %get-tuple-element.212), channel_id=1, replica_groups=mesh['lat'=8,'lon_0'=4,'lon_1'=4,'obs'=2] {'lon_0'}, use_global_device_ids=true, to_apply=%region_29.30 | all-reduce | flops 2 | bytes 16 | tf_op jit(solution)/shard_map/psum | solution.py:29
  469.3 11.9 %all-reduce.7 = (f32[]{:T(128)}, f32[]{:T(128)}) all-reduce(f32[]{:T(128)} %get-tuple-element.231, f32[]{:T(128)} %get-tuple-element.232), channel_id=1, replica_groups=mesh['lat'=8,'lon_0'=4,'lon_1'=4,'obs'=2] {'lon_1'}, use_global_device_ids=true, to_apply=%region_30.31 | all-reduce | flops 2 | bytes 16 | tf_op jit(solution)/shard_map/psum | solution.py:29
  481.2 8.8 %all-reduce.17 = (f32[]{:T(128)}, f32[]{:T(128)}) all-reduce(f32[]{:T(128)} %get-tuple-element.221, f32[]{:T(128)} %get-tuple-element.222), channel_id=1, replica_groups=mesh['lat'=8,'lon_0'=4,'lon_1'=4,'obs'=2] {'obs'}, use_global_device_ids=true, to_apply=%region_31.32 | all-reduce | flops 2 | bytes 16 | tf_op jit(solution)/shard_map/psum | solution.py:29
  494.0 2.0 collective-permute-start.18
  496.7 2.3 collective-permute-done.19
  499.1 4.8 collective-permute-start.21
  503.9 1.6 collective-permute-done.20
  506.4 13.4 %all-reduce.1 = (f32[]{:T(128)}, f32[]{:T(128)}) all-reduce(f32[]{:T(128)} %get-tuple-element.188, f32[]{:T(128)} %get-tuple-element.187), channel_id=1, replica_groups=mesh['lat'=8,'lon_0'=4,'lon_1'=4,'obs'=2] {'lat'}, use_global_device_ids=true, to_apply=%region_38.39 | all-reduce | flops 2 | bytes 16 | tf_op jit(solution)/shard_map/psum | solution.py:29
  519.7 6.6 %all-reduce.11 = (f32[]{:T(128)}, f32[]{:T(128)}) all-reduce(f32[]{:T(128)} %get-tuple-element.209, f32[]{:T(128)} %get-tuple-element.210), channel_id=1, replica_groups=mesh['lat'=8,'lon_0'=4,'lon_1'=4,'obs'=2] {'lon_0'}, use_global_device_ids=true, to_apply=%region_39.40 | all-reduce | flops 2 | bytes 16 | tf_op jit(solution)/shard_map/psum | solution.py:29
  526.3 11.9 %all-reduce.6 = (f32[]{:T(128)}, f32[]{:T(128)}) all-reduce(f32[]{:T(128)} %get-tuple-element.229, f32[]{:T(128)} %get-tuple-element.230), channel_id=1, replica_groups=mesh['lat'=8,'lon_0'=4,'lon_1'=4,'obs'=2] {'lon_1'}, use_global_device_ids=true, to_apply=%region_40.41 | all-reduce | flops 2 | bytes 16 | tf_op jit(solution)/shard_map/psum | solution.py:29
  538.2 9.5 %all-reduce.16 = (f32[]{:T(128)}, f32[]{:T(128)}) all-reduce(f32[]{:T(128)} %get-tuple-element.219, f32[]{:T(128)} %get-tuple-element.220), channel_id=1, replica_groups=mesh['lat'=8,'lon_0'=4,'lon_1'=4,'obs'=2] {'obs'}, use_global_device_ids=true, to_apply=%region_41.42 | all-reduce | flops 2 | bytes 16 | tf_op jit(solution)/shard_map/psum | solution.py:29
  551.6 1.2 collective-permute-start.22
  553.5 2.3 collective-permute-done.23
  555.9 4.8 collective-permute-start.25
  560.7 1.2 collective-permute-done.24
  562.8 14.4 %all-reduce = (f32[]{:T(128)}, f32[]{:T(128)}) all-reduce(f32[]{:T(128)} %get-tuple-element.186, f32[]{:T(128)} %get-tuple-element.185), channel_id=1, replica_groups=mesh['lat'=8,'lon_0'=4,'lon_1'=4,'obs'=2] {'lat'}, use_global_device_ids=true, to_apply=%region_48.49 | all-reduce | flops 2 | bytes 16 | tf_op jit(solution)/shard_map/psum | solution.py:29
  577.1 6.6 %all-reduce.10 = (f32[]{:T(128)}, f32[]{:T(128)}) all-reduce(f32[]{:T(128)} %get-tuple-element.207, f32[]{:T(128)} %get-tuple-element.208), channel_id=1, replica_groups=mesh['lat'=8,'lon_0'=4,'lon_1'=4,'obs'=2] {'lon_0'}, use_global_device_ids=true, to_apply=%region_49.50 | all-reduce | flops 2 | bytes 16 | tf_op jit(solution)/shard_map/psum | solution.py:29
  583.7 11.9 %all-reduce.5 = (f32[]{:T(128)}, f32[]{:T(128)}) all-reduce(f32[]{:T(128)} %get-tuple-element.227, f32[]{:T(128)} %get-tuple-element.228), channel_id=1, replica_groups=mesh['lat'=8,'lon_0'=4,'lon_1'=4,'obs'=2] {'lon_1'}, use_global_device_ids=true, to_apply=%region_50.51 | all-reduce | flops 2 | bytes 16 | tf_op jit(solution)/shard_map/psum | solution.py:29
  595.7 8.8 %all-reduce.15 = (f32[]{:T(128)}, f32[]{:T(128)}) all-reduce(f32[]{:T(128)} %get-tuple-element.217, f32[]{:T(128)} %get-tuple-element.218), channel_id=1, replica_groups=mesh['lat'=8,'lon_0'=4,'lon_1'=4,'obs'=2] {'obs'}, use_global_device_ids=true, to_apply=%region_51.52 | all-reduce | flops 2 | bytes 16 | tf_op jit(solution)/shard_map/psum | solution.py:29
  (155 shorter events, 19.2 us)
Async XLA Ops:
  0.6 20.5 %copy-start.3 = (f32[2,128,128]{2,1,0:T(8,128)S(1)}, f32[2,128,128]{2,1,0:T(8,128)}, u32[]{:S(2)}) copy-start(f32[2,128,128]{2,1,0:T(8,128)} %param.17) | copy-start | bytes 393220
  0.6 20.6 %copy-start.4 = (f32[128,128]{1,0:T(8,128)S(1)}, f32[128,128]{1,0:T(8,128)}, u32[]{:S(2)}) copy-start(f32[128,128]{1,0:T(8,128)} %param.15) | copy-start | bytes 196612
  0.7 20.6 %copy-start.5 = (f32[128,128]{1,0:T(8,128)S(1)}, f32[128,128]{1,0:T(8,128)}, u32[]{:S(2)}) copy-start(f32[128,128]{1,0:T(8,128)} %param.16) | copy-start | bytes 196612
  4.8 28.3 %all-to-all-start = ((s32[128,1,1,3,128]{4,2,3,1,0:T(1,128)}), s32[128,1,1,3,128]{4,2,3,1,0:T(1,128)S(1)}, u32[]{:S(2)}, u32[]{:S(2)}) async-start(s32[128,1,1,3,128]{4,2,3,1,0:T(1,128)} %bitcast.5), calls=%async_computation | async-start | bytes 393216 | tf_op jit(solution)/shard_map/all_to_all | solution.py:51
  33.1 26.9 %all-to-all-start.1 = ((f32[128,1,1,3,3,128]{5,2,4,3,1,0:T(1,128)}), f32[128,1,1,3,3,128]{5,2,4,3,1,0:T(1,128)S(1)}, u32[]{:S(2)}, u32[]{:S(2)}) async-start(f32[128,1,1,3,3,128]{5,2,4,3,1,0:T(1,128)} %copy.29), calls=%async_computation.1 | async-start | bytes 1179648 | tf_op jit(solution)/shard_map/all_to_all | solution.py:51
  297.7 5.8 collective-permute-start
  304.1 12.9 %copy-start.1 = (f32[32,1024]{1,0:T(8,128)S(1)}, f32[32,1024]{1,0:T(8,128)}, u32[]{:S(2)}) copy-start(f32[32,1024]{1,0:T(8,128)} %param.23) | copy-start | bytes 393220
  304.2 12.9 %copy-start.2 = (s32[32,1024]{1,0:T(8,128)S(1)}, s32[32,1024]{1,0:T(8,128)}, u32[]{:S(2)}) copy-start(s32[32,1024]{1,0:T(8,128)} %param.21) | copy-start | bytes 393220
  304.5 3.4 collective-permute-start.1
  317.0 16.3 %copy-start = (f32[32,1024]{1,0:T(8,128)S(1)}, f32[32,1024]{1,0:T(8,128)}, u32[]{:S(2)}) copy-start(f32[32,1024]{1,0:T(8,128)} %param.22) | copy-start | bytes 393220
  317.1 4.0 collective-permute-start.2
  319.4 3.0 collective-permute-start.3
  319.4 7.9 %collective-permute-start.6 = (f32[1,1024]{1,0:T(1,128)S(1)}, f32[1,1024]{1,0:T(1,128)S(1)}, u32[]{:S(2)}, u32[]{:S(2)}) collective-permute-start(f32[1,1024]{1,0:T(1,128)S(1)} %get-tuple-element.291), channel_id=1, source_target_pairs={{0,1},{1,32},{32,33},{33,64},{64,65},{65,96},{96,97},{97,128},{128... | collective-permute-start | bytes 12296 | tf_op jit(solution)/shard_map/ppermute | solution.py:19
  321.1 6.2 %collective-permute-start.7 = (f32[1,1024]{1,0:T(1,128)S(1)}, f32[1,1024]{1,0:T(1,128)S(1)}, u32[]{:S(2)}, u32[]{:S(2)}) collective-permute-start(f32[1,1024]{1,0:T(1,128)S(1)} %get-tuple-element.292), channel_id=1, source_target_pairs={{1,0},{32,1},{33,32},{64,33},{65,64},{96,65},{97,96},{128,97},{129... | collective-permute-start | bytes 12296 | tf_op jit(solution)/shard_map/ppermute | solution.py:22
  322.5 9.7 %collective-permute-start.4 = (f32[34,1]{1,0:T(8,128)S(1)}, f32[34,1]{1,0:T(8,128)S(1)}, u32[]{:S(2)}, u32[]{:S(2)}) collective-permute-start(f32[34,1]{1,0:T(8,128)S(1)} %get-tuple-element.273), channel_id=1, source_target_pairs={{0,2},{2,4},{4,6},{6,8},{8,10},{10,12},{12,14},{14,16},{16,18},{18... | collective-permute-start | bytes 416 | tf_op jit(solution)/shard_map/ppermute | solution.py:19
  322.5 9.7 %collective-permute-start.5 = (f32[34,1]{1,0:T(8,128)S(1)}, f32[34,1]{1,0:T(8,128)S(1)}, u32[]{:S(2)}, u32[]{:S(2)}) collective-permute-start(f32[34,1]{1,0:T(8,128)S(1)} %get-tuple-element.274), channel_id=1, source_target_pairs={{2,0},{4,2},{6,4},{8,6},{10,8},{12,10},{14,12},{16,14},{18,16},{20... | collective-permute-start | bytes 416 | tf_op jit(solution)/shard_map/ppermute | solution.py:22
  327.4 6.0 collective-permute-start.8
  327.4 5.9 collective-permute-start.9
  378.5 2.7 collective-permute-start.10
  380.5 3.0 collective-permute-start.11
  383.6 6.4 %collective-permute-start.12 = (f32[34,1]{1,0:T(8,128)S(1)}, f32[34,1]{1,0:T(8,128)S(1)}, u32[]{:S(2)}, u32[]{:S(2)}) collective-permute-start(f32[34,1]{1,0:T(8,128)S(1)} %get-tuple-element.271), channel_id=1, source_target_pairs={{0,2},{2,4},{4,6},{6,8},{8,10},{10,12},{12,14},{14,16},{16,18},{18... | collective-permute-start | bytes 416 | tf_op jit(solution)/shard_map/ppermute | solution.py:19
  383.6 6.4 %collective-permute-start.13 = (f32[34,1]{1,0:T(8,128)S(1)}, f32[34,1]{1,0:T(8,128)S(1)}, u32[]{:S(2)}, u32[]{:S(2)}) collective-permute-start(f32[34,1]{1,0:T(8,128)S(1)} %get-tuple-element.272), channel_id=1, source_target_pairs={{2,0},{4,2},{6,4},{8,6},{10,8},{12,10},{14,12},{16,14},{18,16},{20... | collective-permute-start | bytes 416 | tf_op jit(solution)/shard_map/ppermute | solution.py:22
  437.1 1.9 collective-permute-start.14
  438.3 3.0 collective-permute-start.15
  441.4 6.0 collective-permute-start.16
  441.4 5.9 collective-permute-start.17
  494.0 2.7 collective-permute-start.18
  496.0 3.0 collective-permute-start.19
  499.1 6.4 %collective-permute-start.20 = (f32[34,1]{1,0:T(8,128)S(1)}, f32[34,1]{1,0:T(8,128)S(1)}, u32[]{:S(2)}, u32[]{:S(2)}) collective-permute-start(f32[34,1]{1,0:T(8,128)S(1)} %get-tuple-element.267), channel_id=1, source_target_pairs={{0,2},{2,4},{4,6},{6,8},{8,10},{10,12},{12,14},{14,16},{16,18},{18... | collective-permute-start | bytes 416 | tf_op jit(solution)/shard_map/ppermute | solution.py:19
  499.1 6.3 %collective-permute-start.21 = (f32[34,1]{1,0:T(8,128)S(1)}, f32[34,1]{1,0:T(8,128)S(1)}, u32[]{:S(2)}, u32[]{:S(2)}) collective-permute-start(f32[34,1]{1,0:T(8,128)S(1)} %get-tuple-element.268), channel_id=1, source_target_pairs={{2,0},{4,2},{6,4},{8,6},{10,8},{12,10},{14,12},{16,14},{18,16},{20... | collective-permute-start | bytes 416 | tf_op jit(solution)/shard_map/ppermute | solution.py:22
  551.6 1.9 collective-permute-start.22
  552.7 3.0 collective-permute-start.23
  555.9 6.0 collective-permute-start.24
  555.9 5.9 collective-permute-start.25
where the time goes:
time: 615 us; the launch traced here: 609 us
  matrix products  225 us (37%)
  blocking collectives  218 us (35%)
  starting transfers between devices  66.1 us (11%)
  waiting for transfers between devices  50 us (8%)
  between operations  19.4 us (3%)
  other arithmetic  10.9 us (2%)
  local copies, waits for them, and re-layouts  10 us (2%)
  loops' own time  9.79 us (2%)
    dot_general x12, matrix products, spread(): jnp.dot(row_weights, col_weights, precision=lax.Precision.HIGHEST, prefer...  225 us
    psum x20, blocking collectives, by_axis(): value = lax.psum(value, axis)  209 us
    ppermute x12, starting transfers between devices, extended(): lax.ppermute(lax.slice_in_dim(block, 0, width, axis=dim), axis, backward)  28.7 us
    all_to_all x2, waiting for transfers between devices, exchange_both(): tiles = lax.all_to_all(tiles, axis, split_axis=0, concat_axis=0, tiled=True)  24.7 us
    all_to_all x2, starting transfers between devices, exchange_both(): tiles = lax.all_to_all(tiles, axis, split_axis=0, concat_axis=0, tiled=True)  23.9 us
  transfers between devices with their start and end apart: 28, of which 18 were waited for; matrix products, arithmetic and copies ran while one was open for 1% of the time, Pallas kernels for 0%

commit v1 on v0

--- a/solution.py
+++ b/solution.py
@@ -26,7 +26,7 @@
 
 def by_axis(value, axes):
     for axis in axes:
-        value = lax.psum(value, axis)
+        value = jnp.sum(lax.all_gather(value, axis), axis=0)
     return value
 
 

time: 615 us -> 677 us (1.10)
  local copies, waits for them, and re-layouts: 10 us -> 67.4 us
  other arithmetic: 10.9 us -> 35.9 us
  blocking collectives: 218 us -> 205 us
  loops' own time: 9.79 us -> 1.43 us
    psum x20 -> x0, blocking collectives: 209 us -> none  [by_axis(): value = lax.psum(value, axis)]
    unnamed x0 -> x20, blocking collectives: none -> 196 us
    unnamed x12 -> x104, local copies, waits for them, and re-layouts: 0.03 us -> 57.4 us
    reduce_sum x0 -> x40, other arithmetic: none -> 24.9 us  [by_axis(): value = jnp.sum(lax.all_gather(value, axis), axis=0)]
    another operation x1, loops' own time: 9.79 us -> 1.43 us  [body(): lax.scan(spread, jnp.zeros((tile_rows + 1, wide), jnp.float32), (scaled_i...]
  transfers between devices with their start and end apart: 28 -> 28, of which waited for: 18 -> 17; matrix products, arithmetic and copies ran while one was open for 1% -> 1% of each run, Pallas kernels for 0% -> 0%
where the time goes in v1:
time: 677 us; the launch traced here: 670 us
  matrix products  225 us (33%)
  blocking collectives  205 us (30%)
  local copies, waits for them, and re-layouts  67.4 us (10%)
  starting transfers between devices  66.3 us (10%)
  waiting for transfers between devices  49.1 us (7%)
  other arithmetic  35.9 us (5%)
  between operations  19.7 us (3%)
    dot_general x12, matrix products, spread(): jnp.dot(row_weights, col_weights, precision=lax.Precision.HIGHEST, prefer...  225 us
    unnamed x20, blocking collectives  196 us
    unnamed x104, local copies, waits for them, and re-layouts  57.4 us
    ppermute x12, starting transfers between devices, extended(): lax.ppermute(lax.slice_in_dim(block, 0, width, axis=dim), axis, backward)  28.8 us
    reduce_sum x40, other arithmetic, by_axis(): value = jnp.sum(lax.all_gather(value, axis), axis=0)  24.9 us
    all_to_all x2, waiting for transfers between devices, exchange_both(): tiles = lax.all_to_all(tiles, axis, split_axis=0, concat_axis=0, tiled=True)  24.7 us
    all_to_all x2, starting transfers between devices, exchange_both(): tiles = lax.all_to_all(tiles, axis, split_axis=0, concat_axis=0, tiled=True)  23.9 us
  transfers between devices with their start and end apart: 28, of which 17 were waited for; matrix products, arithmetic and copies ran while one was open for 1% of the time, Pallas kernels for 0%

profile of v1, /device:TPU:1, one launch (start us, length us, event | category | flops | bytes accessed | tf_op | source)
XLA Modules:
  0.0 670.1 jit_solution(9589041479711257441)
XLA Ops:
  4.8 16.3 %all-to-all-start = ((s32[128,1,1,3,128]{4,2,3,1,0:T(1,128)}), s32[128,1,1,3,128]{4,2,3,1,0:T(1,128)S(1)}, u32[]{:S(2)}, u32[]{:S(2)}) async-start(s32[128,1,1,3,128]{4,2,3,1,0:T(1,128)} %bitcast.5), calls=%async_computation | async-start | bytes 393216 | tf_op jit(solution)/shard_map/all_to_all | solution.py:51
  21.5 4.5 scatter_fusion
  27.6 5.6 all-to-all-done
  33.1 7.6 %all-to-all-start.1 = ((f32[128,1,1,3,3,128]{5,2,4,3,1,0:T(1,128)}), f32[128,1,1,3,3,128]{5,2,4,3,1,0:T(1,128)S(1)}, u32[]{:S(2)}, u32[]{:S(2)}) async-start(f32[128,1,1,3,3,128]{5,2,4,3,1,0:T(1,128)} %copy.29), calls=%async_computation.1 | async-start | bytes 1179648 | tf_op jit(solution)/shard_map/all_to_all | solution.py:51
  40.9 19.1 %all-to-all-done.1 = f32[128,1,1,3,3,128]{5,2,4,3,1,0:T(1,128)S(1)} async-done(((f32[128,1,1,3,3,128]{5,2,4,3,1,0:T(1,128)}), f32[128,1,1,3,3,128]{5,2,4,3,1,0:T(1,128)S(1)}, u32[]{:S(2)}, u32[]{:S(2)}) %all-to-all-start.1) | async-done | bytes 589856 | tf_op jit(solution)/shard_map/all_to_all | solution.py:51
  60.7 228.5 %while.16 = (s32[]{:T(128)}, f32[65,1025]{1,0:T(8,128)S(1)}, s32[12,4096]{1,0:T(8,128)S(1)}, f32[12,4096]{1,0:T(8,128)S(1)}, f32[12,4096]{1,0:T(8,128)S(1)}, /*index=5*/f32[12,4096]{1,0:T(8,128)S(1)}, s32[]{:T(128)}, s32[]{:T(128)}) while((s32[]{:T(128)}, f32[65,1025]{1,0:T(8,128)S(1)}, s32[12,4096]{1,0:T(8,128)S(1)}, ...), condition=%wide.region_4.5_spmd.clone.clone, body=%wide.region_3.4_spmd.clone.clone.sunk | while | flops 3297597440 | bytes 942707 | solution.py:175
  61.4 18.7 %fusion.98 = f32[65,1025]{1,0:T(8,128)S(1)} fusion(f32[4096]{0:T(1024)S(1)} %bitcast.124, s32[4096]{0:T(1024)S(1)} %get-tuple-element.342, f32[4096]{0:T(1024)S(1)} %broadcast_subtract_fusion.5, s32[4096]{0:T(1024)S(1)} %get-tuple-element.343, f32[4096]{0:T(1024)S(1)} %bitcast.131, f32[4096]{0:T(1024)S(1)} %bitcast.130, s32[4096]{0:T(1024)S(1)} %bitcast.132, ...), kind=kOutput, calls=%fused_computation.15.clone.1 | convolution fusion | flops 3297474560 | bytes 680457 | tf_op jit(solution)/shard_map/while/body/eval_jaxpr/dot_general | solution.py:166
  80.4 18.7 %fusion.98 = f32[65,1025]{1,0:T(8,128)S(1)} fusion(f32[4096]{0:T(1024)S(1)} %bitcast.124, s32[4096]{0:T(1024)S(1)} %get-tuple-element.342, f32[4096]{0:T(1024)S(1)} %broadcast_subtract_fusion.5, s32[4096]{0:T(1024)S(1)} %get-tuple-element.343, f32[4096]{0:T(1024)S(1)} %bitcast.131, f32[4096]{0:T(1024)S(1)} %bitcast.130, s32[4096]{0:T(1024)S(1)} %bitcast.132, ...), kind=kOutput, calls=%fused_computation.15.clone.1 | convolution fusion | flops 3297474560 | bytes 680457 | tf_op jit(solution)/shard_map/while/body/eval_jaxpr/dot_general | solution.py:166
  99.4 18.7 %fusion.98 = f32[65,1025]{1,0:T(8,128)S(1)} fusion(f32[4096]{0:T(1024)S(1)} %bitcast.124, s32[4096]{0:T(1024)S(1)} %get-tuple-element.342, f32[4096]{0:T(1024)S(1)} %broadcast_subtract_fusion.5, s32[4096]{0:T(1024)S(1)} %get-tuple-element.343, f32[4096]{0:T(1024)S(1)} %bitcast.131, f32[4096]{0:T(1024)S(1)} %bitcast.130, s32[4096]{0:T(1024)S(1)} %bitcast.132, ...), kind=kOutput, calls=%fused_computation.15.clone.1 | convolution fusion | flops 3297474560 | bytes 680457 | tf_op jit(solution)/shard_map/while/body/eval_jaxpr/dot_general | solution.py:166
  118.3 18.7 %fusion.98 = f32[65,1025]{1,0:T(8,128)S(1)} fusion(f32[4096]{0:T(1024)S(1)} %bitcast.124, s32[4096]{0:T(1024)S(1)} %get-tuple-element.342, f32[4096]{0:T(1024)S(1)} %broadcast_subtract_fusion.5, s32[4096]{0:T(1024)S(1)} %get-tuple-element.343, f32[4096]{0:T(1024)S(1)} %bitcast.131, f32[4096]{0:T(1024)S(1)} %bitcast.130, s32[4096]{0:T(1024)S(1)} %bitcast.132, ...), kind=kOutput, calls=%fused_computation.15.clone.1 | convolution fusion | flops 3297474560 | bytes 680457 | tf_op jit(solution)/shard_map/while/body/eval_jaxpr/dot_general | solution.py:166
  137.3 18.7 %fusion.98 = f32[65,1025]{1,0:T(8,128)S(1)} fusion(f32[4096]{0:T(1024)S(1)} %bitcast.124, s32[4096]{0:T(1024)S(1)} %get-tuple-element.342, f32[4096]{0:T(1024)S(1)} %broadcast_subtract_fusion.5, s32[4096]{0:T(1024)S(1)} %get-tuple-element.343, f32[4096]{0:T(1024)S(1)} %bitcast.131, f32[4096]{0:T(1024)S(1)} %bitcast.130, s32[4096]{0:T(1024)S(1)} %bitcast.132, ...), kind=kOutput, calls=%fused_computation.15.clone.1 | convolution fusion | flops 3297474560 | bytes 680457 | tf_op jit(solution)/shard_map/while/body/eval_jaxpr/dot_general | solution.py:166
  156.3 18.7 %fusion.98 = f32[65,1025]{1,0:T(8,128)S(1)} fusion(f32[4096]{0:T(1024)S(1)} %bitcast.124, s32[4096]{0:T(1024)S(1)} %get-tuple-element.342, f32[4096]{0:T(1024)S(1)} %broadcast_subtract_fusion.5, s32[4096]{0:T(1024)S(1)} %get-tuple-element.343, f32[4096]{0:T(1024)S(1)} %bitcast.131, f32[4096]{0:T(1024)S(1)} %bitcast.130, s32[4096]{0:T(1024)S(1)} %bitcast.132, ...), kind=kOutput, calls=%fused_computation.15.clone.1 | convolution fusion | flops 3297474560 | bytes 680457 | tf_op jit(solution)/shard_map/while/body/eval_jaxpr/dot_general | solution.py:166
  175.3 18.7 %fusion.98 = f32[65,1025]{1,0:T(8,128)S(1)} fusion(f32[4096]{0:T(1024)S(1)} %bitcast.124, s32[4096]{0:T(1024)S(1)} %get-tuple-element.342, f32[4096]{0:T(1024)S(1)} %broadcast_subtract_fusion.5, s32[4096]{0:T(1024)S(1)} %get-tuple-element.343, f32[4096]{0:T(1024)S(1)} %bitcast.131, f32[4096]{0:T(1024)S(1)} %bitcast.130, s32[4096]{0:T(1024)S(1)} %bitcast.132, ...), kind=kOutput, calls=%fused_computation.15.clone.1 | convolution fusion | flops 3297474560 | bytes 680457 | tf_op jit(solution)/shard_map/while/body/eval_jaxpr/dot_general | solution.py:166
  194.3 18.7 %fusion.98 = f32[65,1025]{1,0:T(8,128)S(1)} fusion(f32[4096]{0:T(1024)S(1)} %bitcast.124, s32[4096]{0:T(1024)S(1)} %get-tuple-element.342, f32[4096]{0:T(1024)S(1)} %broadcast_subtract_fusion.5, s32[4096]{0:T(1024)S(1)} %get-tuple-element.343, f32[4096]{0:T(1024)S(1)} %bitcast.131, f32[4096]{0:T(1024)S(1)} %bitcast.130, s32[4096]{0:T(1024)S(1)} %bitcast.132, ...), kind=kOutput, calls=%fused_computation.15.clone.1 | convolution fusion | flops 3297474560 | bytes 680457 | tf_op jit(solution)/shard_map/while/body/eval_jaxpr/dot_general | solution.py:166
  213.3 18.7 %fusion.98 = f32[65,1025]{1,0:T(8,128)S(1)} fusion(f32[4096]{0:T(1024)S(1)} %bitcast.124, s32[4096]{0:T(1024)S(1)} %get-tuple-element.342, f32[4096]{0:T(1024)S(1)} %broadcast_subtract_fusion.5, s32[4096]{0:T(1024)S(1)} %get-tuple-element.343, f32[4096]{0:T(1024)S(1)} %bitcast.131, f32[4096]{0:T(1024)S(1)} %bitcast.130, s32[4096]{0:T(1024)S(1)} %bitcast.132, ...), kind=kOutput, calls=%fused_computation.15.clone.1 | convolution fusion | flops 3297474560 | bytes 680457 | tf_op jit(solution)/shard_map/while/body/eval_jaxpr/dot_general | solution.py:166
  232.3 18.7 %fusion.98 = f32[65,1025]{1,0:T(8,128)S(1)} fusion(f32[4096]{0:T(1024)S(1)} %bitcast.124, s32[4096]{0:T(1024)S(1)} %get-tuple-element.342, f32[4096]{0:T(1024)S(1)} %broadcast_subtract_fusion.5, s32[4096]{0:T(1024)S(1)} %get-tuple-element.343, f32[4096]{0:T(1024)S(1)} %bitcast.131, f32[4096]{0:T(1024)S(1)} %bitcast.130, s32[4096]{0:T(1024)S(1)} %bitcast.132, ...), kind=kOutput, calls=%fused_computation.15.clone.1 | convolution fusion | flops 3297474560 | bytes 680457 | tf_op jit(solution)/shard_map/while/body/eval_jaxpr/dot_general | solution.py:166
  251.3 18.7 %fusion.98 = f32[65,1025]{1,0:T(8,128)S(1)} fusion(f32[4096]{0:T(1024)S(1)} %bitcast.124, s32[4096]{0:T(1024)S(1)} %get-tuple-element.342, f32[4096]{0:T(1024)S(1)} %broadcast_subtract_fusion.5, s32[4096]{0:T(1024)S(1)} %get-tuple-element.343, f32[4096]{0:T(1024)S(1)} %bitcast.131, f32[4096]{0:T(1024)S(1)} %bitcast.130, s32[4096]{0:T(1024)S(1)} %bitcast.132, ...), kind=kOutput, calls=%fused_computation.15.clone.1 | convolution fusion | flops 3297474560 | bytes 680457 | tf_op jit(solution)/shard_map/while/body/eval_jaxpr/dot_general | solution.py:166
  270.3 18.7 %fusion.98 = f32[65,1025]{1,0:T(8,128)S(1)} fusion(f32[4096]{0:T(1024)S(1)} %bitcast.124, s32[4096]{0:T(1024)S(1)} %get-tuple-element.342, f32[4096]{0:T(1024)S(1)} %broadcast_subtract_fusion.5, s32[4096]{0:T(1024)S(1)} %get-tuple-element.343, f32[4096]{0:T(1024)S(1)} %bitcast.131, f32[4096]{0:T(1024)S(1)} %bitcast.130, s32[4096]{0:T(1024)S(1)} %bitcast.132, ...), kind=kOutput, calls=%fused_computation.15.clone.1 | convolution fusion | flops 3297474560 | bytes 680457 | tf_op jit(solution)/shard_map/while/body/eval_jaxpr/dot_general | solution.py:166
  290.6 4.5 collective-permute-done
  296.1 2.7 collective-permute-start.1
  299.6 9.0 %all_to_all.15 = f32[2,32,1024]{2,1,0:T(8,128)S(1)} all-to-all(f32[2,32,1024]{2,1,0:T(8,128)S(1)} %bitcast.127), channel_id=1, replica_groups=mesh['lat'=8,'lon_0'=4,'lon_1'=4,'obs'=2] {'obs'}, dimensions={0} | all-to-all | bytes 524288 | tf_op jit(solution)/shard_map/all_to_all | solution.py:70
  308.8 2.3 collective-permute-start.2
  311.1 1.7 collective-permute-start.6
  314.2 4.8 collective-permute-start.5
  319.1 4.8 collective-permute-start.9
  326.0 1.4 dynamic-update-slice.10
  327.4 1.4 dynamic-update-slice.6
  329.4 12.5 %all-reduce.44 = (f32[8]{0:T(128)S(1)}, f32[8]{0:T(128)S(1)}) all-reduce(f32[8]{0:T(128)S(1)} %dynamic-update-slice.6, f32[8]{0:T(128)S(1)} %dynamic-update-slice.10), channel_id=1, replica_groups=mesh['lat'=8,'lon_0'=4,'lon_1'=4,'obs'=2] {'lat'}, use_global_device_ids=true, to_apply=%add | all-reduce | flops 16 | bytes 128
  346.5 6.0 all-reduce.54
  356.9 11.0 %all-reduce.49 = (f32[4]{0:T(128)S(1)}, f32[4]{0:T(128)S(1)}) all-reduce(f32[4]{0:T(128)S(1)} %dynamic-update-slice.8, f32[4]{0:T(128)S(1)} %dynamic-update-slice.12), channel_id=1, replica_groups=mesh['lat'=8,'lon_0'=4,'lon_1'=4,'obs'=2] {'lon_1'}, use_global_device_ids=true, to_apply=%add.2 | all-reduce | flops 8 | bytes 64
  371.9 10.8 %all-reduce.59 = (f32[2]{0:T(128)S(1)}, f32[2]{0:T(128)S(1)}) all-reduce(f32[2]{0:T(128)S(1)} %dynamic-update-slice.9, f32[2]{0:T(128)S(1)} %dynamic-update-slice.13), channel_id=1, replica_groups=mesh['lat'=8,'lon_0'=4,'lon_1'=4,'obs'=2] {'obs'}, use_global_device_ids=true, to_apply=%add.3 | all-reduce | flops 4 | bytes 32
  385.3 2.0 collective-permute-start.10
  388.1 2.3 collective-permute-done.11
  390.4 4.8 collective-permute-start.13
  395.2 1.6 collective-permute-done.12
  399.2 1.4 dynamic-update-slice.14
  400.6 12.6 %all-reduce.43 = (f32[8]{0:T(128)S(1)}, f32[8]{0:T(128)S(1)}) all-reduce(f32[8]{0:T(128)S(1)} %dynamic-update-slice.14, f32[8]{0:T(128)S(1)} %dynamic-update-slice.18), channel_id=1, replica_groups=mesh['lat'=8,'lon_0'=4,'lon_1'=4,'obs'=2] {'lat'}, use_global_device_ids=true, to_apply=%add.8 | all-reduce | flops 16 | bytes 128
  417.2 6.0 all-reduce.53
  427.0 11.2 %all-reduce.48 = (f32[4]{0:T(128)S(1)}, f32[4]{0:T(128)S(1)}) all-reduce(f32[4]{0:T(128)S(1)} %dynamic-update-slice.16, f32[4]{0:T(128)S(1)} %dynamic-update-slice.20), channel_id=1, replica_groups=mesh['lat'=8,'lon_0'=4,'lon_1'=4,'obs'=2] {'lon_1'}, use_global_device_ids=true, to_apply=%add.10 | all-reduce | flops 8 | bytes 64
  442.1 8.9 %all-reduce.58 = (f32[2]{0:T(128)S(1)}, f32[2]{0:T(128)S(1)}) all-reduce(f32[2]{0:T(128)S(1)} %dynamic-update-slice.17, f32[2]{0:T(128)S(1)} %dynamic-update-slice.21), channel_id=1, replica_groups=mesh['lat'=8,'lon_0'=4,'lon_1'=4,'obs'=2] {'obs'}, use_global_device_ids=true, to_apply=%add.11 | all-reduce | flops 4 | bytes 32
  458.8 2.3 collective-permute-done.15
  461.2 5.0 collective-permute-start.17
  468.1 1.4 dynamic-update-slice.26
  469.5 1.4 dynamic-update-slice.22
  471.0 13.7 %all-reduce.42 = (f32[8]{0:T(128)S(1)}, f32[8]{0:T(128)S(1)}) all-reduce(f32[8]{0:T(128)S(1)} %dynamic-update-slice.22, f32[8]{0:T(128)S(1)} %dynamic-update-slice.26), channel_id=1, replica_groups=mesh['lat'=8,'lon_0'=4,'lon_1'=4,'obs'=2] {'lat'}, use_global_device_ids=true, to_apply=%add.16 | all-reduce | flops 16 | bytes 128
  488.7 6.0 all-reduce.52
  498.5 11.5 %all-reduce.47 = (f32[4]{0:T(128)S(1)}, f32[4]{0:T(128)S(1)}) all-reduce(f32[4]{0:T(128)S(1)} %dynamic-update-slice.24, f32[4]{0:T(128)S(1)} %dynamic-update-slice.28), channel_id=1, replica_groups=mesh['lat'=8,'lon_0'=4,'lon_1'=4,'obs'=2] {'lon_1'}, use_global_device_ids=true, to_apply=%add.18 | all-reduce | flops 8 | bytes 64
  514.0 8.2 %all-reduce.57 = (f32[2]{0:T(128)S(1)}, f32[2]{0:T(128)S(1)}) all-reduce(f32[2]{0:T(128)S(1)} %dynamic-update-slice.25, f32[2]{0:T(128)S(1)} %dynamic-update-slice.29), channel_id=1, replica_groups=mesh['lat'=8,'lon_0'=4,'lon_1'=4,'obs'=2] {'obs'}, use_global_device_ids=true, to_apply=%add.19 | all-reduce | flops 4 | bytes 32
  527.4 1.9 collective-permute-start.18
  530.1 2.3 collective-permute-done.19
  532.5 4.8 collective-permute-start.21
  537.2 1.5 collective-permute-done.20
  539.7 1.4 dynamic-update-slice.34
  542.6 12.7 %all-reduce.41 = (f32[8]{0:T(128)S(1)}, f32[8]{0:T(128)S(1)}) all-reduce(f32[8]{0:T(128)S(1)} %dynamic-update-slice.30, f32[8]{0:T(128)S(1)} %dynamic-update-slice.34), channel_id=1, replica_groups=mesh['lat'=8,'lon_0'=4,'lon_1'=4,'obs'=2] {'lat'}, use_global_device_ids=true, to_apply=%add.24 | all-reduce | flops 16 | bytes 128
  559.4 6.0 all-reduce.51
  569.3 11.3 %all-reduce.46 = (f32[4]{0:T(128)S(1)}, f32[4]{0:T(128)S(1)}) all-reduce(f32[4]{0:T(128)S(1)} %dynamic-update-slice.32, f32[4]{0:T(128)S(1)} %dynamic-update-slice.36), channel_id=1, replica_groups=mesh['lat'=8,'lon_0'=4,'lon_1'=4,'obs'=2] {'lon_1'}, use_global_device_ids=true, to_apply=%add.26 | all-reduce | flops 8 | bytes 64
  584.7 8.8 %all-reduce.56 = (f32[2]{0:T(128)S(1)}, f32[2]{0:T(128)S(1)}) all-reduce(f32[2]{0:T(128)S(1)} %dynamic-update-slice.33, f32[2]{0:T(128)S(1)} %dynamic-update-slice.37), channel_id=1, replica_groups=mesh['lat'=8,'lon_0'=4,'lon_1'=4,'obs'=2] {'obs'}, use_global_device_ids=true, to_apply=%add.27 | all-reduce | flops 4 | bytes 32
  600.8 2.3 collective-permute-done.23
  603.2 4.8 collective-permute-start.25
  610.1 1.4 dynamic-update-slice.42
  612.9 13.6 %all-reduce.40 = (f32[8]{0:T(128)S(1)}, f32[8]{0:T(128)S(1)}) all-reduce(f32[8]{0:T(128)S(1)} %dynamic-update-slice.38, f32[8]{0:T(128)S(1)} %dynamic-update-slice.42), channel_id=1, replica_groups=mesh['lat'=8,'lon_0'=4,'lon_1'=4,'obs'=2] {'lat'}, use_global_device_ids=true, to_apply=%add.32 | all-reduce | flops 16 | bytes 128
  630.5 6.0 all-reduce.50
  640.4 10.9 %all-reduce.45 = (f32[4]{0:T(128)S(1)}, f32[4]{0:T(128)S(1)}) all-reduce(f32[4]{0:T(128)S(1)} %dynamic-update-slice.40, f32[4]{0:T(128)S(1)} %dynamic-update-slice.44), channel_id=1, replica_groups=mesh['lat'=8,'lon_0'=4,'lon_1'=4,'obs'=2] {'lon_1'}, use_global_device_ids=true, to_apply=%add.34 | all-reduce | flops 8 | bytes 64
  655.2 8.6 %all-reduce.55 = (f32[2]{0:T(128)S(1)}, f32[2]{0:T(128)S(1)}) all-reduce(f32[2]{0:T(128)S(1)} %dynamic-update-slice.41, f32[2]{0:T(128)S(1)} %dynamic-update-slice.45), channel_id=1, replica_groups=mesh['lat'=8,'lon_0'=4,'lon_1'=4,'obs'=2] {'obs'}, use_global_device_ids=true, to_apply=%add.35 | all-reduce | flops 4 | bytes 32
  (287 shorter events, 99.4 us)
Async XLA Ops:
  0.6 20.5 %copy-start.3 = (f32[2,128,128]{2,1,0:T(8,128)S(1)}, f32[2,128,128]{2,1,0:T(8,128)}, u32[]{:S(2)}) copy-start(f32[2,128,128]{2,1,0:T(8,128)} %param.17) | copy-start | bytes 393220
  0.6 20.6 %copy-start.4 = (f32[128,128]{1,0:T(8,128)S(1)}, f32[128,128]{1,0:T(8,128)}, u32[]{:S(2)}) copy-start(f32[128,128]{1,0:T(8,128)} %param.15) | copy-start | bytes 196612
  0.7 20.6 %copy-start.5 = (f32[128,128]{1,0:T(8,128)S(1)}, f32[128,128]{1,0:T(8,128)}, u32[]{:S(2)}) copy-start(f32[128,128]{1,0:T(8,128)} %param.16) | copy-start | bytes 196612
  4.8 28.3 %all-to-all-start = ((s32[128,1,1,3,128]{4,2,3,1,0:T(1,128)}), s32[128,1,1,3,128]{4,2,3,1,0:T(1,128)S(1)}, u32[]{:S(2)}, u32[]{:S(2)}) async-start(s32[128,1,1,3,128]{4,2,3,1,0:T(1,128)} %bitcast.5), calls=%async_computation | async-start | bytes 393216 | tf_op jit(solution)/shard_map/all_to_all | solution.py:51
  33.1 26.9 %all-to-all-start.1 = ((f32[128,1,1,3,3,128]{5,2,4,3,1,0:T(1,128)}), f32[128,1,1,3,3,128]{5,2,4,3,1,0:T(1,128)S(1)}, u32[]{:S(2)}, u32[]{:S(2)}) async-start(f32[128,1,1,3,3,128]{5,2,4,3,1,0:T(1,128)} %copy.29), calls=%async_computation.1 | async-start | bytes 1179648 | tf_op jit(solution)/shard_map/all_to_all | solution.py:51
  289.3 5.8 collective-permute-start
  290.3 8.4 %copy-start.9 = (u32[256]{0:T(256)S(1)}, u32[256]{0:T(256)}, u32[]{:S(2)}) copy-start(u32[256]{0:T(256)} %constant.148) | copy-start | bytes 3076
  295.9 12.8 %copy-start.1 = (f32[32,1024]{1,0:T(8,128)S(1)}, f32[32,1024]{1,0:T(8,128)}, u32[]{:S(2)}) copy-start(f32[32,1024]{1,0:T(8,128)} %param.23) | copy-start | bytes 393220
  295.9 12.8 %copy-start.2 = (s32[32,1024]{1,0:T(8,128)S(1)}, s32[32,1024]{1,0:T(8,128)}, u32[]{:S(2)}) copy-start(s32[32,1024]{1,0:T(8,128)} %param.21) | copy-start | bytes 393220
  296.1 3.4 collective-permute-start.1
  308.7 16.4 %copy-start = (f32[32,1024]{1,0:T(8,128)S(1)}, f32[32,1024]{1,0:T(8,128)}, u32[]{:S(2)}) copy-start(f32[32,1024]{1,0:T(8,128)} %param.22) | copy-start | bytes 393220
  308.7 20.1 %copy-start.8 = (u32[256]{0:T(256)S(1)}, u32[256]{0:T(256)}, u32[]{:S(2)}) copy-start(u32[256]{0:T(256)} %constant.153) | copy-start | bytes 3076
  308.7 37.2 %copy-start.7 = (u32[256]{0:T(256)S(1)}, u32[256]{0:T(256)}, u32[]{:S(2)}) copy-start(u32[256]{0:T(256)} %constant.158) | copy-start | bytes 3076
  308.7 47.6 %copy-start.6 = (u32[256]{0:T(256)S(1)}, u32[256]{0:T(256)}, u32[]{:S(2)}) copy-start(u32[256]{0:T(256)} %constant.163) | copy-start | bytes 3076
  308.8 4.0 collective-permute-start.2
  311.0 3.0 collective-permute-start.3
  311.1 7.9 %collective-permute-start.6 = (f32[1,1024]{1,0:T(1,128)S(1)}, f32[1,1024]{1,0:T(1,128)S(1)}, u32[]{:S(2)}, u32[]{:S(2)}) collective-permute-start(f32[1,1024]{1,0:T(1,128)S(1)} %get-tuple-element.291), channel_id=1, source_target_pairs={{0,1},{1,32},{32,33},{33,64},{64,65},{65,96},{96,97},{97,128},{128... | collective-permute-start | bytes 12296 | tf_op jit(solution)/shard_map/ppermute | solution.py:19
  312.8 6.2 collective-permute-start.7
  314.2 9.7 %collective-permute-start.4 = (f32[34,1]{1,0:T(8,128)S(1)}, f32[34,1]{1,0:T(8,128)S(1)}, u32[]{:S(2)}, u32[]{:S(2)}) collective-permute-start(f32[34,1]{1,0:T(8,128)S(1)} %get-tuple-element.273), channel_id=1, source_target_pairs={{0,2},{2,4},{4,6},{6,8},{8,10},{10,12},{12,14},{14,16},{16,18},{18... | collective-permute-start | bytes 416 | tf_op jit(solution)/shard_map/ppermute | solution.py:19
  314.2 9.7 %collective-permute-start.5 = (f32[34,1]{1,0:T(8,128)S(1)}, f32[34,1]{1,0:T(8,128)S(1)}, u32[]{:S(2)}, u32[]{:S(2)}) collective-permute-start(f32[34,1]{1,0:T(8,128)S(1)} %get-tuple-element.274), channel_id=1, source_target_pairs={{2,0},{4,2},{6,4},{8,6},{10,8},{12,10},{14,12},{16,14},{18,16},{20... | collective-permute-start | bytes 416 | tf_op jit(solution)/shard_map/ppermute | solution.py:22
  319.0 6.0 collective-permute-start.8
  319.1 5.9 collective-permute-start.9
  385.3 2.7 collective-permute-start.10
  387.3 3.0 collective-permute-start.11
  390.4 6.4 collective-permute-start.12
  390.4 6.4 collective-permute-start.13
  456.8 1.9 collective-permute-start.14
  458.0 3.0 collective-permute-start.15
  461.1 6.0 collective-permute-start.16
  461.2 5.9 collective-permute-start.17
  527.4 2.7 collective-permute-start.18
  529.3 3.0 collective-permute-start.19
  532.4 6.3 collective-permute-start.20
  532.5 6.3 collective-permute-start.21
  598.7 2.0 collective-permute-start.22
  600.0 3.0 collective-permute-start.23
  603.1 6.0 collective-permute-start.24
  603.2 5.9 collective-permute-start.25
